TPU v7x, 32 devices: a whole 2x2x4 slice. The times are simulated.
32 devices in a mesh: shard: 2 (over core), ctx: 4 (over y, x), tp: 4 (over z).
Axes of the slice: x: 2, y: 2, z: 4, core: 2. Of those that a mesh axis runs over, the one named last changes fastest.
Arguments:
- layer_input: bfloat16 [8, 1024, 2048], P('shard', 'ctx'), may hold values from -6 to 6
- output_gradient: bfloat16 [8, 1024, 2048], P('shard', 'ctx'), may hold values from -6 to 6
- picture_piece_starts: int32 [8, 2], P('shard'), may hold values from 0 to 768, as said below
- sequence_adapter_index: int32 [8], P('shard'), may hold values from 0 to 7
- attention_norm_gain: float32 [2048], replicated, may hold values from 0.5 to 1.5
- attention_norm_bias: float32 [2048], replicated, may hold values from -1 to 1
- feedforward_norm_gain: float32 [2048], replicated, may hold values from 0.5 to 1.5
- feedforward_norm_bias: float32 [2048], replicated, may hold values from -1 to 1
- query_key_value_weight: bfloat16 [2048, 3, 2048], P('shard', None, 'tp'), may hold values from -0.125 to 0.125
- attention_output_weight: bfloat16 [2048, 2048], P('tp', 'shard'), may hold values from -0.375 to 0.375
- up_projection_weight: bfloat16 [2048, 8192], P('shard', 'tp'), may hold values from -0.125 to 0.125
- down_projection_weight: bfloat16 [8192, 2048], P('tp', 'shard'), may hold values from -0.09375 to 0.09375
- adapter_projection_first: bfloat16 [8, 2048, 16], replicated, may hold values from -0.125 to 0.125
- adapter_projection_second: bfloat16 [8, 16, 3, 2048], P(None, None, None, 'tp'), may hold values from -0.75 to 0.75
- adapter_heads_first: bfloat16 [8, 2048, 16], P(None, 'tp'), may hold values from -0.375 to 0.375
- adapter_heads_second: bfloat16 [8, 16, 2048], replicated, may hold values from -0.75 to 0.75
- adapter_up_first: bfloat16 [8, 2048, 16], replicated, may hold values from -0.125 to 0.125
- adapter_up_second: bfloat16 [8, 16, 8192], P(None, None, 'tp'), may hold values from -0.75 to 0.75
- adapter_down_first: bfloat16 [8, 8192, 16], P(None, 'tp'), may hold values from -0.09375 to 0.09375
- adapter_down_second: bfloat16 [8, 16, 2048], replicated, may hold values from -0.75 to 0.75
Outputs:
- layer_out: bfloat16 [8, 1024, 2048], P('shard', 'ctx')
- input_grad: bfloat16 [8, 1024, 2048], P('shard', 'ctx')
- qkv_in_grad: float32 [8, 2048, 16], replicated
- qkv_out_grad: float32 [8, 16, 3, 2048], P(None, None, None, 'tp')
- heads_in_grad: float32 [8, 2048, 16], P(None, 'tp')
- heads_out_grad: float32 [8, 16, 2048], replicated
- up_in_grad: float32 [8, 2048, 16], replicated
- up_out_grad: float32 [8, 16, 8192], P(None, None, 'tp')
- down_in_grad: float32 [8, 8192, 16], P(None, 'tp')
- down_out_grad: float32 [8, 16, 2048], replicated
Inputs may be any that keep to these rules, and one draw needn't show every extreme that they name: `picture_piece_starts`: piece c of a sequence starts within positions c * 512 to (c + 1) * 512 - 256, so pieces never meet; in some sequence a piece starts at 0, in some sequence a piece ends at 1024.
All inputs are finite; a program needn't handle non-finite values.
Results may differ from a plain program's by a relative error of at most 0.019.
Values may be sent and summed in bfloat16 or wider, within the bound.
A program may use at most 320 MiB of HBM per device.

v0:
```python
import jax
import jax.numpy as jnp
from jax import lax
from jax.sharding import PartitionSpec as P

HD = 128
PIC = 256
NORM_EPS = 1e-05


def layer_norm(inputs, gains, biases):
    average = jnp.mean(inputs, axis=-1, keepdims=True)
    centred = inputs - average
    spread = jnp.mean(centred * centred, axis=-1, keepdims=True)
    return centred * lax.rsqrt(spread + NORM_EPS) * gains + biases


def gelu_tanh(inputs):
    return (
        0.5
        * inputs
        * (1.0 + jnp.tanh(0.7978845608028654 * (inputs + 0.044715 * inputs * inputs * inputs)))
    )


def flattened_first(adapter_mat):
    adapter_tables, inner_dim, rank_width = adapter_mat.shape
    return jnp.transpose(adapter_mat, (1, 0, 2)).reshape(inner_dim, adapter_tables * rank_width)


def flattened_second(adapter_mat):
    return adapter_mat.reshape(adapter_mat.shape[0] * adapter_mat.shape[1], -1)


def unflat_in(grad_flat, adapter_tables):
    inner_dim = grad_flat.shape[0]
    return jnp.transpose(grad_flat.reshape(inner_dim, adapter_tables, -1), (1, 0, 2))


def matmul(left_mat, right_mat):
    return jnp.dot(left_mat, right_mat, preferred_element_type=jnp.float32)


def matmul_tn(left_mat, right_mat):
    return lax.dot_general(
        left_mat, right_mat, (((0,), (0,)), ((), ())), preferred_element_type=jnp.float32
    )


def matmul_nt(left_mat, right_mat):
    return lax.dot_general(
        left_mat, right_mat, (((1,), (1,)), ((), ())), preferred_element_type=jnp.float32
    )


def piece_labels(starts, positions):
    inside = (positions[None, None, :] >= starts[:, :, None]) & (
        positions[None, None, :] < starts[:, :, None] + PIC
    )
    labels = jnp.arange(1, starts.shape[1] + 1, dtype=jnp.int32)
    return jnp.sum(jnp.where(inside, labels[None, :, None], 0), axis=1)


def visible(query_pos, key_pos, query_labels, key_labels):
    causal = key_pos[None, None, :] <= query_pos[None, :, None]
    shared = (query_labels[:, :, None] == key_labels[:, None, :]) & (query_labels[:, :, None] > 0)
    return causal | shared


def exponents(queries, key_rows, query_pos, key_pos, visible_mask, slopes):
    score_scale = queries.shape[-1] ** (-0.5)
    logits = (
        jnp.einsum("sqhd,skhd->shqk", queries, key_rows, preferred_element_type=jnp.float32)
        * score_scale
    )
    distance = jnp.abs(query_pos[:, None] - key_pos[None, :]).astype(jnp.float32)
    logits = logits - slopes[None, :, None, None] * distance[None, None]
    return jnp.where(visible_mask[:, None], jnp.exp(logits), 0.0)


def block_grads(
    queries, scaled_grad, row_delta, key_rows, value_rows, query_pos, key_pos, visible_mask, slopes
):
    score_scale = queries.shape[-1] ** (-0.5)
    exponent = exponents(queries, key_rows, query_pos, key_pos, visible_mask, slopes)
    products_gv = jnp.einsum(
        "sqhd,skhd->shqk", scaled_grad, value_rows, preferred_element_type=jnp.float32
    )
    grad_logits = (
        exponent * (products_gv - jnp.transpose(row_delta, (0, 2, 1))[..., None])
    ).astype(jnp.bfloat16)
    grad_queries = (
        jnp.einsum("shqk,skhd->sqhd", grad_logits, key_rows, preferred_element_type=jnp.float32)
        * score_scale
    )
    grad_keyrows = (
        jnp.einsum("shqk,sqhd->skhd", grad_logits, queries, preferred_element_type=jnp.float32)
        * score_scale
    )
    grad_valrows = jnp.einsum(
        "shqk,sqhd->skhd",
        exponent.astype(jnp.bfloat16),
        scaled_grad,
        preferred_element_type=jnp.float32,
    )
    return (grad_queries, grad_keyrows, grad_valrows)


def reduce_heads(partials):
    return lax.psum((partials[0], partials[1]), "tp")


def body(
    layer_input,
    output_gradient,
    picture_piece_starts,
    sequence_adapter_index,
    attention_norm_gain,
    attention_norm_bias,
    feedforward_norm_gain,
    feedforward_norm_bias,
    query_key_value_weight,
    attention_output_weight,
    up_projection_weight,
    down_projection_weight,
    adapter_projection_first,
    adapter_projection_second,
    adapter_heads_first,
    adapter_heads_second,
    adapter_up_first,
    adapter_up_second,
    adapter_down_first,
    adapter_down_second,
):
    seq_here, local_len, model_width = layer_input.shape
    tok_rows = seq_here * local_len
    adapter_tables = adapter_projection_first.shape[0]
    rank_width = adapter_projection_first.shape[2]
    head_width = HD
    device_heads = adapter_projection_second.shape[-1] // head_width
    local_width = device_heads * head_width
    columns = jnp.arange(adapter_tables * rank_width, dtype=jnp.int32) // rank_width
    chosen = (sequence_adapter_index[:, None] == columns[None, :]).astype(jnp.float32)
    select = jnp.broadcast_to(
        chosen[:, None, :], (seq_here, local_len, adapter_tables * rank_width)
    ).reshape(tok_rows, adapter_tables * rank_width)
    head_ids = lax.axis_index("tp") * device_heads + jnp.arange(device_heads, dtype=jnp.int32)
    slopes = jnp.exp2(
        -8.0 * (head_ids.astype(jnp.float32) + 1.0) / (device_heads * lax.axis_size("tp"))
    )
    here_pos = lax.axis_index("ctx") * local_len + jnp.arange(local_len, dtype=jnp.int32)
    here_labels = piece_labels(picture_piece_starts, here_pos)
    projection_first_flattened = flattened_first(adapter_projection_first)
    projection_second_flattened = flattened_second(adapter_projection_second)
    heads_first_flattened = flattened_first(adapter_heads_first)
    heads_second_flattened = flattened_second(adapter_heads_second)
    up_first_flattened = flattened_first(adapter_up_first)
    up_second_flattened = flattened_second(adapter_up_second)
    down_first_flattened = flattened_first(adapter_down_first)
    down_second_flattened = flattened_second(adapter_down_second)
    residual = layer_input.reshape(tok_rows, model_width).astype(jnp.float32)
    first_norm, first_back_full = jax.vjp(
        lambda inputs: layer_norm(inputs, attention_norm_gain, attention_norm_bias), residual
    )
    first_act = first_norm.astype(jnp.bfloat16)
    gathered_rows = (
        lax.all_gather(query_key_value_weight, "shard", axis=0, tiled=True),
        lax.all_gather(up_projection_weight, "shard", axis=0, tiled=True),
    )
    qkv_full = gathered_rows[0].reshape(model_width, 3 * local_width)
    up_full = gathered_rows[1]
    gathered_cols = (
        lax.all_gather(attention_output_weight, "shard", axis=1, tiled=True),
        lax.all_gather(down_projection_weight, "shard", axis=1, tiled=True),
    )
    heads_full = gathered_cols[0]
    down_full = gathered_cols[1]
    first_low = (matmul(first_act, projection_first_flattened) * select).astype(jnp.bfloat16)
    projected = (
        matmul(first_act, qkv_full) + matmul(first_low, projection_second_flattened)
    ).astype(jnp.bfloat16)
    queries_flat = projected[:, :local_width].reshape(seq_here, local_len, local_width)
    queries = queries_flat.reshape(seq_here, local_len, device_heads, head_width)
    key_rows = projected[:, local_width : 2 * local_width].reshape(seq_here, local_len, local_width)
    value_rows = projected[:, 2 * local_width :].reshape(seq_here, local_len, local_width)
    pieces = (
        lax.all_gather(key_rows, "ctx", axis=1, tiled=True),
        lax.all_gather(value_rows, "ctx", axis=1, tiled=True),
    )
    piece_len = pieces[0].shape[1]
    key_pos = jnp.arange(piece_len, dtype=jnp.int32)
    key_labels = piece_labels(picture_piece_starts, key_pos)
    visible_mask = visible(here_pos, key_pos, here_labels, key_labels)
    piece_keys = pieces[0].reshape(seq_here, piece_len, device_heads, head_width)
    piece_values = pieces[1].reshape(seq_here, piece_len, device_heads, head_width)
    exponent = exponents(queries, piece_keys, here_pos, key_pos, visible_mask, slopes)
    weighted = jnp.einsum(
        "shqk,skhd->sqhd",
        exponent.astype(jnp.bfloat16),
        piece_values,
        preferred_element_type=jnp.float32,
    )
    weighted, totals = (weighted, jnp.sum(exponent, axis=-1))
    per_total = jnp.transpose(totals, (0, 2, 1))[..., None]
    heads_raw = weighted / per_total
    heads_act = heads_raw.reshape(tok_rows, local_width).astype(jnp.bfloat16)
    heads_part = matmul(heads_act, heads_full)
    heads_low_part = matmul(heads_act, heads_first_flattened)
    attn_total, attn_low_total = reduce_heads((heads_part, heads_low_part))
    heads_low_here = (attn_low_total * select).astype(jnp.bfloat16)
    middle_here = residual + attn_total + matmul(heads_low_here, heads_second_flattened)
    second_norm, second_back = jax.vjp(
        lambda inputs: layer_norm(inputs, feedforward_norm_gain, feedforward_norm_bias), middle_here
    )
    second_act_here = second_norm.astype(jnp.bfloat16)
    up_low_here = (matmul(second_act_here, up_first_flattened) * select).astype(jnp.bfloat16)
    second_act, up_low, heads_low = (second_act_here, up_low_here, heads_low_here)
    hidden = matmul(second_act, up_full) + matmul(up_low, up_second_flattened)
    activated, gelu_back = jax.vjp(gelu_tanh, hidden)
    activated = activated.astype(jnp.bfloat16)
    down_part = matmul(activated, down_full)
    down_low_part = matmul(activated, down_first_flattened)
    ffn_total, ffn_low_total = reduce_heads((down_part, down_low_part))
    down_low_here = (ffn_low_total * select).astype(jnp.bfloat16)
    result_here = (middle_here + ffn_total + matmul(down_low_here, down_second_flattened)).astype(
        jnp.bfloat16
    )
    grad_top_low = output_gradient.reshape(tok_rows, model_width)
    grad_top = grad_top_low.astype(jnp.float32)
    down_back = (matmul_nt(grad_top_low, down_second_flattened) * select).astype(jnp.bfloat16)
    grad_down_in = matmul_tn(activated, down_back)
    grad_activated = matmul_nt(grad_top_low, down_full) + matmul_nt(down_back, down_first_flattened)
    grad_hidden = gelu_back(grad_activated)[0].astype(jnp.bfloat16)
    up_second_gradient = matmul_tn(up_low, grad_hidden)
    ffn_back_part = matmul_nt(grad_hidden, up_full)
    ffn_back_low = matmul_nt(grad_hidden, up_second_flattened)
    back_total, back_low_total = reduce_heads((ffn_back_part, ffn_back_low))
    up_back_here = (back_low_total * select).astype(jnp.bfloat16)
    grad_second = back_total + matmul_nt(up_back_here, up_first_flattened)
    grad_middle_here = grad_top + second_back(grad_second)[0]
    grad_middle_low_here = grad_middle_here.astype(jnp.bfloat16)
    heads_back_here = (matmul_nt(grad_middle_low_here, heads_second_flattened) * select).astype(
        jnp.bfloat16
    )
    result_rows, down_low, grad_middle_low, heads_back, up_back = (
        result_here,
        down_low_here,
        grad_middle_low_here,
        heads_back_here,
        up_back_here,
    )
    layer_out = result_rows.reshape(layer_input.shape)
    down_second_gradient = matmul_tn(down_low, grad_top_low)
    grad_up_in = matmul_tn(second_act, up_back)
    heads_second_gradient = matmul_tn(heads_low, grad_middle_low)
    grad_heads_in = matmul_tn(heads_act, heads_back)
    grad_heads = (
        matmul_nt(grad_middle_low, heads_full) + matmul_nt(heads_back, heads_first_flattened)
    ).astype(jnp.bfloat16)
    grad_heads_wide = grad_heads.reshape(seq_here, local_len, device_heads, head_width).astype(
        jnp.float32
    )
    scaled_grad = (grad_heads_wide / per_total).astype(jnp.bfloat16)
    row_delta = jnp.sum(grad_heads_wide * heads_raw, axis=-1) / per_total[..., 0]
    pieces = (
        lax.all_gather(key_rows, "ctx", axis=1, tiled=True),
        lax.all_gather(value_rows, "ctx", axis=1, tiled=True),
    )
    piece_len = pieces[0].shape[1]
    key_pos = jnp.arange(piece_len, dtype=jnp.int32)
    key_labels = piece_labels(picture_piece_starts, key_pos)
    visible_mask = visible(here_pos, key_pos, here_labels, key_labels)
    piece_keys = pieces[0].reshape(seq_here, piece_len, device_heads, head_width)
    piece_values = pieces[1].reshape(seq_here, piece_len, device_heads, head_width)
    grad_queries, grad_keyrows, grad_valrows = block_grads(
        queries,
        scaled_grad,
        row_delta,
        piece_keys,
        piece_values,
        here_pos,
        key_pos,
        visible_mask,
        slopes,
    )
    grad_keys_all, grad_values_all = (
        lax.psum_scatter(grad_keyrows, "ctx", scatter_dimension=1, tiled=True),
        lax.psum_scatter(grad_valrows, "ctx", scatter_dimension=1, tiled=True),
    )
    grad_projected = jnp.concatenate(
        [
            grad_queries.reshape(tok_rows, local_width),
            grad_keys_all.reshape(tok_rows, local_width),
            grad_values_all.reshape(tok_rows, local_width),
        ],
        axis=1,
    ).astype(jnp.bfloat16)
    projection_second_gradient = matmul_tn(first_low, grad_projected)
    attn_back_part = matmul_nt(grad_projected, qkv_full)
    attn_back_low = matmul_nt(grad_projected, projection_second_flattened)
    first_total, first_low_total = reduce_heads((attn_back_part, attn_back_low))
    qkv_back_here = (first_low_total * select).astype(jnp.bfloat16)
    grad_first = first_total + matmul_nt(qkv_back_here, projection_first_flattened)
    input_here = (grad_middle_here + first_back_full(grad_first)[0]).astype(jnp.bfloat16)
    input_rows, qkv_back = (input_here, qkv_back_here)
    input_grad = input_rows.reshape(layer_input.shape)
    grad_qkv_in = matmul_tn(first_act, qkv_back)
    adapter_terms = (
        unflat_in(grad_qkv_in, adapter_tables),
        projection_second_gradient.reshape(adapter_projection_second.shape),
        unflat_in(grad_heads_in, adapter_tables),
        heads_second_gradient.reshape(adapter_heads_second.shape),
        unflat_in(grad_up_in, adapter_tables),
        up_second_gradient.reshape(adapter_up_second.shape),
        unflat_in(grad_down_in, adapter_tables),
        down_second_gradient.reshape(adapter_down_second.shape),
    )
    summed = lax.psum(
        (
            adapter_terms[0],
            adapter_terms[1],
            adapter_terms[2],
            adapter_terms[3],
            adapter_terms[4],
            adapter_terms[5],
            adapter_terms[6],
            adapter_terms[7],
        ),
        ("shard", "ctx"),
    )
    return (
        layer_out,
        input_grad,
        summed[0],
        summed[1],
        summed[2],
        summed[3],
        summed[4],
        summed[5],
        summed[6],
        summed[7],
    )


def solution(mesh):
    placed = (
        P("shard", "ctx", None),
        P("shard", "ctx", None),
        P("shard", None),
        P("shard"),
        P(),
        P(),
        P(),
        P(),
        P("shard", None, "tp"),
        P("tp", "shard"),
        P("shard", "tp"),
        P("tp", "shard"),
        P(),
        P(None, None, None, "tp"),
        P(None, "tp", None),
        P(),
        P(),
        P(None, None, "tp"),
        P(None, "tp", None),
        P(),
    )
    return jax.shard_map(
        body,
        mesh=mesh,
        in_specs=placed,
        out_specs=(
            P("shard", "ctx", None),
            P("shard", "ctx", None),
            P(),
            P(None, None, None, "tp"),
            P(None, "tp", None),
            P(),
            P(),
            P(None, None, "tp"),
            P(None, "tp", None),
            P(),
        ),
        check_vma=False,
    )
```

profile of v0, /device:TPU:0, one launch (start us, length us, event | category | flops | bytes accessed | tf_op | source)
XLA Modules:
  0.0 1857.7 jit_solution(7738910371380799832)
XLA Ops:
  7.3 4.7 copy.69
  12.6 3.2 convert_reduce_fusion
  23.4 8.2 all-gather.7.cloned.1.call-done
  31.6 10.1 fusion.54
  47.8 2.6 broadcast_multiply_fusion
  54.1 43.8 %all-gather.9.cloned.1.call-done = bf16[4,1024,512]{2,1,0:T(8,128)(2,1)} async-done(((bf16[4,256,512]{2,1,0:T(8,128)(2,1)}), bf16[4,1024,512]{2,1,0:T(8,128)(2,1)}) %all-gather.9.cloned.1.call-update) | async-done | bytes 4194320 | tf_op jit(solution)/shard_map/all_gather | solution.py:188
  97.9 6.3 copy.71
  104.2 48.5 %all-gather.11.cloned.1.call-done = bf16[4,1024,512]{1,2,0:T(8,128)(2,1)} async-done(((bf16[4,256,512]{1,2,0:T(8,128)(2,1)}), bf16[4,1024,512]{1,2,0:T(8,128)(2,1)}) %all-gather.11.cloned.1.call-update) | async-done | bytes 4194320 | tf_op jit(solution)/shard_map/all_gather | solution.py:187
  152.8 12.5 fusion.51
  165.3 10.2 fusion.52
  177.4 7.6 fusion.34
  186.1 3.4 fusion.30
  189.6 14.8 fusion.58
  204.4 294.8 %all-reduce.15.cloned.1.call-done = (f32[1024,2048]{1,0:T(8,128)}, f32[1024,128]{1,0:T(8,128)}) async-done(((f32[1024,2048]{1,0:T(8,128)}, f32[1024,128]{1,0:T(8,128)}), (f32[1024,2048]{1,0:T(8,128)}, f32[1024,128]{1,0:T(8,128)})) %all-reduce.15.cloned.1.call-update) | async-done | bytes 8912912 | tf_op jit(solution)/shard_map/psum | solution.py:110
  500.3 6.3 fusion.53
  514.4 5.2 all-gather.15.cloned.1.call-done
  519.6 12.5 fusion.55
  532.1 4.9 multiply_convert_fusion.1
  537.0 9.4 fusion.3
  548.6 11.2 fusion.59
  559.8 309.0 %all-reduce.13.cloned.1.call-done = (f32[1024,2048]{1,0:T(8,128)}, f32[1024,128]{1,0:T(8,128)}) async-done(((f32[1024,2048]{1,0:T(8,128)}, f32[1024,128]{1,0:T(8,128)}), (f32[1024,2048]{1,0:T(8,128)}, f32[1024,128]{1,0:T(8,128)})) %all-reduce.13.cloned.1.call-update) | async-done | bytes 8912912 | tf_op jit(solution)/shard_map/psum | solution.py:110
  869.9 7.4 multiply_reduce_fusion
  877.4 4.8 fusion.48
  882.2 3.6 fusion.16
  886.8 3.4 fusion.31
  890.3 5.2 fusion.61
  901.5 8.6 multiply_convert_fusion
  910.1 3.2 copy-done.9
  913.3 4.9 multiply_bitcast_fusion
  918.4 10.6 fusion.21
  930.1 4.5 fusion.57
  934.6 14.9 fusion.56
  949.5 2.9 fusion.27
  954.3 49.3 %reduce-scatter.3.cloned.1.call-done = f32[4,256,4,128]{1,3,2,0:T(8,128)} async-done(((f32[4,1024,4,128]{1,3,2,0:T(8,128)}), f32[4,256,4,128]{1,3,2,0:T(8,128)}) %reduce-scatter.3.cloned.1.call-update) | async-done | bytes 2097168 | tf_op jit(solution)/shard_map/reduce_scatter | solution.py:287
  1006.1 86.9 %reduce-scatter.5.cloned.1.call-done = f32[4,256,4,128]{1,3,2,0:T(8,128)} async-done(((f32[4,1024,4,128]{1,3,2,0:T(8,128)}), f32[4,256,4,128]{1,3,2,0:T(8,128)}) %reduce-scatter.5.cloned.1.call-update) | async-done | bytes 2097168 | tf_op jit(solution)/shard_map/reduce_scatter | solution.py:288
  1099.7 3.6 fusion.63
  1103.3 11.8 fusion.62
  1116.7 3.9 fusion.67
  1120.7 4.5 fusion.68
  1126.3 4.2 fusion.66
  1132.3 2.6 fusion.64
  1136.4 575.2 %all-reduce.11.cloned.1.call-done = (f32[1024,2048]{1,0:T(8,128)}, f32[1024,128]{1,0:T(8,128)}, f32[1024,2048]{1,0:T(8,128)}, f32[1024,128]{1,0:T(8,128)}) async-done(((f32[1024,2048]{1,0:T(8,128)}, f32[1024,128]{1,0:T(8,128)}, f32[1024,2048]{1,0:T(8,128)}, f32[1024,128]{1,0:T(8,128)}), (f32[1024,2048]{1,0:T(8,128)}, f32[1024,128]{1,0:T(8,128)}, f32[1024,2048]{1,0:T(8,128)}, ...) | async-done | bytes 17825808 | tf_op jit(solution)/shard_map/psum | solution.py:110
  1713.2 4.0 convolution_bitcast_fusion
  1719.1 8.5 fusion.10
  1728.4 5.8 fusion.47
  1734.2 7.1 add_convert_fusion.1
  1741.4 7.2 add_convert_fusion
  1748.6 88.1 %all-reduce.9.cloned.1.call-done = (f32[8,2048,16]{1,2,0:T(8,128)}, f32[8,16,3,512]{3,2,1,0:T(4,128)}, f32[8,512,16]{1,2,0:T(8,128)}, f32[8,16,2048]{2,1,0:T(8,1...) async-done(((f32[8,2048,16]{1,2,0:T(8,128)}, f32[8,16,3,512]{3,2,1,0:T(4,128)}, ...) | async-done | bytes 7340048 | tf_op jit(solution)/shard_map/psum | solution.py:318
  (223 shorter events, 76.2 us)
Async XLA Ops:
  7.2 524.9 %copy-start = (bf16[8,16,2048]{2,1,0:T(8,128)(2,1)S(1)}, bf16[8,16,2048]{2,1,0:T(8,128)(2,1)}, u32[]{:S(2)}) copy-start(bf16[8,16,2048]{2,1,0:T(8,128)(2,1)} %param.37) | copy-start | bytes 1572868
  7.2 11.1 copy-start.45
  7.2 11.1 copy-start.51
  7.2 24.4 %all-gather.7.cloned.1.call-start = ((), (), s32[]{:S(2)}) async-start(), calls=%async_computation.2 | async-start | bytes 9437184 | tf_op jit(solution)/shard_map/all_gather | solution.py:167
  12.0 85.9 %all-gather.9.cloned.1.call-start = ((), (), s32[]{:S(2)}) async-start(), calls=%async_computation.3 | async-start | bytes 5242880 | tf_op jit(solution)/shard_map/all_gather | solution.py:188
  12.5 29.2 %copy-start.20 = (bf16[16,8,3,512]{3,1,2,0:T(8,128)(2,1)}, bf16[16,8,3,512]{3,1,2,0:T(8,128)(2,1)S(1)}, u32[]{:S(2)}) copy-start(bf16[16,8,3,512]{3,1,2,0:T(8,128)(2,1)S(1)} %copy.93) | copy-start | bytes 1179652
  12.6 856.2 %copy-start.40 = (f32[4,128]{1,0:T(4,128)}, f32[4,128]{1,0:T(4,128)S(1)}, u32[]{:S(2)}) copy-start(f32[4,128]{1,0:T(4,128)S(1)} %compare_convert_fusion) | copy-start | bytes 6148
  12.6 9.5 copy-start.28
  23.4 18.3 copy-start.24
  44.0 108.8 %all-gather.11.cloned.1.call-start = ((), (), s32[]{:S(2)}) async-start(), calls=%async_computation.4 | async-start | bytes 5242880 | tf_op jit(solution)/shard_map/all_gather | solution.py:187
  45.4 132.1 %all-gather.13.cloned.1.call-start = ((), (), s32[]{:S(2)}) async-start(), calls=%async_computation.5 | async-start | bytes 3145728 | tf_op jit(solution)/shard_map/all_gather | solution.py:173
  45.9 143.6 %all-gather.17.cloned.1.call-start = ((), (), s32[]{:S(2)}) async-start(), calls=%async_computation.7 | async-start | bytes 12582912 | tf_op jit(solution)/shard_map/all_gather | solution.py:174
  46.5 452.7 %all-reduce.15.cloned.1.call-start = ((), (), s32[]{:S(2)}) async-start(), calls=%async_computation.13 | async-start | bytes 17825792 | tf_op jit(solution)/shard_map/psum | solution.py:110
  54.1 111.2 %copy-start.16 = (bf16[4,256,4,128]{1,3,2,0:T(8,128)(2,1)}, bf16[4,256,4,128]{1,3,2,0:T(8,128)(2,1)S(1)}, u32[]{:S(2)}) copy-start(bf16[4,256,4,128]{1,3,2,0:T(8,128)(2,1)S(1)} %copy.82) | copy-start | bytes 3145732
  152.8 12.5 copy-start.10
  165.3 10.9 copy-start.38
  176.2 8.9 copy-start.18
  185.1 334.5 %all-gather.15.cloned.1.call-start = ((), (), s32[]{:S(2)}) async-start(), calls=%async_computation.6 | async-start | bytes 12582912 | tf_op jit(solution)/shard_map/all_gather | solution.py:168
  185.9 683.0 %all-reduce.13.cloned.1.call-start = ((), (), s32[]{:S(2)}) async-start(), calls=%async_computation.12 | async-start | bytes 17825792 | tf_op jit(solution)/shard_map/psum | solution.py:110
  189.5 310.7 %copy-start.27 = (bf16[8,16,2048]{2,1,0:T(8,128)(2,1)S(1)}, bf16[8,16,2048]{2,1,0:T(8,128)(2,1)}, u32[]{:S(2)}) copy-start(bf16[8,16,2048]{2,1,0:T(8,128)(2,1)} %param.35) | copy-start | bytes 1572868
  500.3 6.3 copy-start.22
  507.6 5.5 copy-start.26
  514.4 17.7 copy-start.34
  532.1 16.4 slice-start.6
  537.0 11.6 slice-start.7
  559.7 443.9 %reduce-scatter.3.cloned.1.call-start = ((), (), s32[]{:S(2)}) async-start(), calls=%async_computation.8 | async-start | bytes 10485760 | tf_op jit(solution)/shard_map/reduce_scatter | solution.py:287
  901.5 11.8 copy-start.17
  918.2 174.7 %reduce-scatter.5.cloned.1.call-start = ((), (), s32[]{:S(2)}) async-start(), calls=%async_computation.9 | async-start | bytes 10485760 | tf_op jit(solution)/shard_map/reduce_scatter | solution.py:288
  929.1 782.5 %all-reduce.11.cloned.1.call-start = ((), (), s32[]{:S(2)}) async-start(), calls=%async_computation.11 | async-start | bytes 35651584 | tf_op jit(solution)/shard_map/psum | solution.py:110
  930.1 19.4 %slice-start.4 = ((s8[8388608]{0:T(1024)(128)(4,1)}), s8[4194304]{0:T(1024)(128)(4,1)S(1)}, s32[]{:S(2)}) async-start(s8[8388608]{0:T(1024)(128)(4,1)} %bitcast.208), calls=%async_computation.18 | async-start | bytes 8388608
  934.6 14.9 slice-start.5
  934.6 15.0 copy-start.14
  953.1 146.5 %copy-start.21 = (bf16[16,8,3,512]{3,1,2,0:T(8,128)(2,1)S(1)}, bf16[16,8,3,512]{3,1,2,0:T(8,128)(2,1)}, u32[]{:S(2)}) copy-start(bf16[16,8,3,512]{3,1,2,0:T(8,128)(2,1)} %copy-done.20) | copy-start | bytes 1179652
  1115.1 721.6 %all-reduce.9.cloned.1.call-start = ((), (), s32[]{:S(2)}) async-start(), calls=%async_computation.10 | async-start | bytes 15204352 | tf_op jit(solution)/shard_map/psum | solution.py:318
  1120.7 9.9 copy-start.23
  1125.2 7.2 copy-start.25
  1126.3 585.3 %copy-start.42 = (f32[4,128]{1,0:T(4,128)S(1)}, f32[4,128]{1,0:T(4,128)}, u32[]{:S(2)}) copy-start(f32[4,128]{1,0:T(4,128)} %copy-done.40) | copy-start | bytes 6148
  1719.0 15.2 slice-start
  1719.0 9.3 copy-start.4
  1719.0 15.1 slice-start.1
  1728.4 13.0 slice-start.2
  1734.2 7.2 copy-start.7
  1734.2 7.2 slice-start.3
  1734.2 7.1 copy-start.44
  1741.4 109.3 %copy-start.1 = (bf16[8,16,2048]{2,1,0:T(8,128)(2,1)S(1)}, bf16[8,16,2048]{2,1,0:T(8,128)(2,1)}, u32[]{:S(2)}) copy-start(bf16[8,16,2048]{2,1,0:T(8,128)(2,1)} %param.37) | copy-start | bytes 1572868
  1836.7 11.1 copy-start.33
  1836.7 12.0 copy-start.32
  1836.7 13.0 copy-start.31
  (26 other events, 77.8 us)
Sparse Core Ops, SparseCore 0:
  12.1 19.4 all-gather.6
  44.1 53.7 all-gather.8
  100.3 52.4 all-gather.10
  154.2 10.5 all-gather.12
  166.1 21.0 all-gather.16
  190.2 308.9 all-reduce.14
  500.7 18.8 all-gather.14
  559.9 308.9 all-reduce.12
  918.3 85.2 reduce-scatter.2
  1006.6 86.3 reduce-scatter.4
  1115.2 596.3 all-reduce.10
  1719.1 117.4 all-reduce.8
where the time goes:
time: 1870 us; the launch traced here: 1860 us
  waiting for transfers between devices  1510 us (81%)
  matrix products  227 us (12%)
  local copies, waits for them, and re-layouts  58 us (3%)
  other arithmetic  44.6 us (2%)
    psum x3, waiting for transfers between devices, reduce_heads(): return lax.psum((partials[0], partials[1]), 'tp')  1180 us
    psum x1, waiting for transfers between devices, body(): lax.psum((adapter_terms[0], adapter_terms[1], adapter_terms[2], adapter_t...  88.1 us
    reduce_scatter x1, waiting for transfers between devices, body(): lax.psum_scatter(grad_valrows, 'ctx', scatter_dimension=1, tiled=True)  86.9 us
    dot_general x12, matrix products, matmul_nt(): lax.dot_general(left_mat, right_mat, (((1,), (1,)), ((), ())), preferred_...  81.3 us
    dot_general x12, matrix products, matmul(): return jnp.dot(left_mat, right_mat, preferred_element_type=jnp.float32)  72.6 us
    reduce_scatter x1, waiting for transfers between devices, body(): lax.psum_scatter(grad_keyrows, 'ctx', scatter_dimension=1, tiled=True)  49.3 us
    all_gather x1, waiting for transfers between devices, body(): lax.all_gather(key_rows, 'ctx', axis=1, tiled=True)  48.5 us
    all_gather x1, waiting for transfers between devices, body(): lax.all_gather(value_rows, 'ctx', axis=1, tiled=True)  43.8 us
  transfers between devices with their start and end apart: 12, of which 10 were waited for; matrix products, arithmetic and copies ran while one was open for 9% of the time, Pallas kernels for 0%

commit v1 on v0

--- a/solution.py
+++ b/solution.py
@@ -6,6 +6,28 @@
 HD = 128
 PIC = 256
 NORM_EPS = 1e-05
+
+
+def in_order(blocks, dim):
+    shape = list(blocks.shape[1:])
+    shape[dim] *= blocks.shape[0]
+    return jnp.moveaxis(blocks, 0, dim).reshape(shape)
+
+
+def collected_by_bits(x, axis):
+    size = lax.axis_size(axis)
+    blocks = x[None]
+    for level in range(size.bit_length() - 1):
+        bit = 1 << level
+        other = lax.ppermute(blocks, axis, [(i, i ^ bit) for i in range(size)])
+        both = jnp.stack([blocks, other])
+        upper = lax.axis_index(axis) >> level & 1
+        blocks = jnp.where(upper == 0, both, both[::-1]).reshape(-1, *x.shape)
+    return blocks
+
+
+def gather_by_bits(shard, axis, dim):
+    return in_order(collected_by_bits(shard, axis), dim)
 
 
 def layer_norm(inputs, gains, biases):
@@ -185,7 +207,7 @@
     value_rows = projected[:, 2 * local_width :].reshape(seq_here, local_len, local_width)
     pieces = (
         lax.all_gather(key_rows, "ctx", axis=1, tiled=True),
-        lax.all_gather(value_rows, "ctx", axis=1, tiled=True),
+        gather_by_bits(value_rows, "ctx", 1),
     )
     piece_len = pieces[0].shape[1]
     key_pos = jnp.arange(piece_len, dtype=jnp.int32)

time: 1870 us -> 1890 us (1.011)
    ppermute x0 -> x2, waiting for transfers between devices: none -> 92.3 us  [collected_by_bits(): other = lax.ppermute(blocks, axis, [(i, i ^ bit) for i in range(size)])]
    all_gather x1, waiting for transfers between devices: 48.5 us -> 0.01 us  [body(): lax.all_gather(key_rows, 'ctx', axis=1, tiled=True)]
    reduce_scatter x1, waiting for transfers between devices: 86.9 us -> 47.1 us  [body(): lax.psum_scatter(grad_valrows, 'ctx', scatter_dimension=1, tiled=True)]
    reduce_scatter x1, waiting for transfers between devices: 49.3 us -> 86.9 us  [body(): lax.psum_scatter(grad_keyrows, 'ctx', scatter_dimension=1, tiled=True)]
    all_gather x1, waiting for transfers between devices: 43.8 us -> 9.73 us  [body(): lax.all_gather(value_rows, 'ctx', axis=1, tiled=True)]
  transfers between devices with their start and end apart: 12 -> 14, of which waited for: 10 -> 11; matrix products, arithmetic and copies ran while one was open for 9% -> 13% of each run, Pallas kernels for 0% -> 0%
where the time goes in v1:
time: 1890 us; the launch traced here: 1880 us
  waiting for transfers between devices  1510 us (80%)
  matrix products  227 us (12%)
  local copies, waits for them, and re-layouts  71 us (4%)
  other arithmetic  56.2 us (3%)
    psum x3, waiting for transfers between devices, reduce_heads(): return lax.psum((partials[0], partials[1]), 'tp')  1170 us
    ppermute x2, waiting for transfers between devices, collected_by_bits(): other = lax.ppermute(blocks, axis, [(i, i ^ bit) for i in range(size)])  92.3 us
    psum x1, waiting for transfers between devices, body(): lax.psum((adapter_terms[0], adapter_terms[1], adapter_terms[2], adapter_t...  88.2 us
    reduce_scatter x1, waiting for transfers between devices, body(): lax.psum_scatter(grad_keyrows, 'ctx', scatter_dimension=1, tiled=True)  86.9 us
    dot_general x12, matrix products, matmul_nt(): lax.dot_general(left_mat, right_mat, (((1,), (1,)), ((), ())), preferred_...  80.5 us
    dot_general x12, matrix products, matmul(): return jnp.dot(left_mat, right_mat, preferred_element_type=jnp.float32)  72.2 us
    reduce_scatter x1, waiting for transfers between devices, body(): lax.psum_scatter(grad_valrows, 'ctx', scatter_dimension=1, tiled=True)  47.1 us
  transfers between devices with their start and end apart: 14, of which 11 were waited for; matrix products, arithmetic and copies ran while one was open for 13% of the time, Pallas kernels for 0%

profile of v1, /device:TPU:0, one launch (start us, length us, event | category | flops | bytes accessed | tf_op | source)
XLA Modules:
  0.0 1884.2 jit_solution(2002894273677613180)
XLA Ops:
  7.3 4.7 copy.69
  12.6 3.2 convert_reduce_fusion
  23.4 8.2 all-gather.7.cloned.1.call-done
  31.6 10.1 fusion.56
  49.9 35.0 %collective-permute-done = bf16[1,4,256,512]{3,2,1,0:T(8,128)(2,1)} collective-permute-done((bf16[1,4,256,512]{3,2,1,0:T(8,128)(2,1)S(1)}, bf16[1,4,256,512]{3,2,1,0:T(8,128)(2,1)}, u32[]{:S(2)}, u32[]{:S(2)}) %collective-permute-start) | collective-permute-done | bytes 1048608 | tf_op jit(solution)/shard_map/ppermute | solution.py:22
  98.4 57.3 %collective-permute-done.1 = bf16[2,4,256,512]{3,2,1,0:T(8,128)(2,1)} collective-permute-done((bf16[2,4,256,512]{3,2,1,0:T(8,128)(2,1)}, bf16[2,4,256,512]{3,2,1,0:T(8,128)(2,1)}, u32[]{:S(2)}, u32[]{:S(2)}) %collective-permute-start.1) | collective-permute-done | bytes 2097184 | tf_op jit(solution)/shard_map/ppermute | solution.py:22
  155.7 3.2 pad_maximum_fusion
  161.9 7.5 copy.71
  169.4 7.7 reshape_reshape.6
  177.1 12.7 fusion.53
  189.9 10.6 fusion.54
  203.3 7.2 fusion.36
  211.6 3.4 fusion.32
  215.1 15.4 fusion.60
  230.5 288.3 %all-reduce.15.cloned.1.call-done = (f32[1024,2048]{1,0:T(8,128)}, f32[1024,128]{1,0:T(8,128)}) async-done(((f32[1024,2048]{1,0:T(8,128)}, f32[1024,128]{1,0:T(8,128)}), (f32[1024,2048]{1,0:T(8,128)}, f32[1024,128]{1,0:T(8,128)})) %all-reduce.15.cloned.1.call-update) | async-done | bytes 8912912 | tf_op jit(solution)/shard_map/psum | solution.py:132
  519.8 6.3 fusion.55
  534.0 5.0 all-gather.13.cloned.1.call-done
  539.0 12.5 fusion.57
  551.5 4.9 multiply_convert_fusion.1
  556.4 9.4 fusion.3
  567.9 11.0 fusion.61
  580.4 307.7 %all-reduce.13.cloned.1.call-done = (f32[1024,2048]{1,0:T(8,128)}, f32[1024,128]{1,0:T(8,128)}) async-done(((f32[1024,2048]{1,0:T(8,128)}, f32[1024,128]{1,0:T(8,128)}), (f32[1024,2048]{1,0:T(8,128)}, f32[1024,128]{1,0:T(8,128)})) %all-reduce.13.cloned.1.call-update) | async-done | bytes 8912912 | tf_op jit(solution)/shard_map/psum | solution.py:132
  889.2 7.4 multiply_reduce_fusion
  896.7 5.4 fusion.50
  902.8 3.7 fusion.16
  906.7 3.4 fusion.33
  910.2 5.2 fusion.63
  919.6 10.7 fusion.21
  932.2 9.7 all-gather.17.cloned.1.call-done
  941.9 8.7 multiply_convert_fusion
  950.7 3.4 copy-done.9
  954.1 4.9 multiply_bitcast_fusion
  960.0 4.6 fusion.59
  964.7 14.8 fusion.58
  979.5 2.9 fusion.29
  984.3 47.1 %reduce-scatter.5.cloned.1.call-done = f32[4,256,4,128]{1,3,2,0:T(8,128)} async-done(((f32[4,1024,4,128]{1,3,2,0:T(8,128)}), f32[4,256,4,128]{1,3,2,0:T(8,128)}) %reduce-scatter.5.cloned.1.call-update) | async-done | bytes 2097168 | tf_op jit(solution)/shard_map/reduce_scatter | solution.py:310
  1033.8 86.9 %reduce-scatter.3.cloned.1.call-done = f32[4,256,4,128]{1,3,2,0:T(8,128)} async-done(((f32[4,1024,4,128]{1,3,2,0:T(8,128)}), f32[4,256,4,128]{1,3,2,0:T(8,128)}) %reduce-scatter.3.cloned.1.call-update) | async-done | bytes 2097168 | tf_op jit(solution)/shard_map/reduce_scatter | solution.py:309
  1127.4 12.4 fusion.64
  1143.4 3.9 fusion.69
  1147.4 4.3 fusion.70
  1152.9 4.2 fusion.67
  1163.0 575.1 %all-reduce.11.cloned.1.call-done = (f32[1024,2048]{1,0:T(8,128)}, f32[1024,128]{1,0:T(8,128)}, f32[1024,2048]{1,0:T(8,128)}, f32[1024,128]{1,0:T(8,128)}) async-done(((f32[1024,2048]{1,0:T(8,128)}, f32[1024,128]{1,0:T(8,128)}, f32[1024,2048]{1,0:T(8,128)}, f32[1024,128]{1,0:T(8,128)}), (f32[1024,2048]{1,0:T(8,128)}, f32[1024,128]{1,0:T(8,128)}, f32[1024,2048]{1,0:T(8,128)}, ...) | async-done | bytes 17825808 | tf_op jit(solution)/shard_map/psum | solution.py:132
  1739.7 4.0 convolution_bitcast_fusion
  1745.5 8.5 fusion.10
  1754.8 5.8 fusion.49
  1760.7 7.1 add_convert_fusion.1
  1767.8 7.2 add_convert_fusion
  1775.0 88.2 %all-reduce.9.cloned.1.call-done = (f32[8,2048,16]{1,2,0:T(8,128)}, f32[8,16,3,512]{3,2,1,0:T(4,128)}, f32[8,512,16]{1,2,0:T(8,128)}, f32[8,16,2048]{2,1,0:T(8,1...) async-done(((f32[8,2048,16]{1,2,0:T(8,128)}, f32[8,16,3,512]{3,2,1,0:T(4,128)}, ...) | async-done | bytes 7340048 | tf_op jit(solution)/shard_map/psum | solution.py:340
  (245 shorter events, 97.9 us)
Async XLA Ops:
  7.2 544.3 %copy-start = (bf16[8,16,2048]{2,1,0:T(8,128)(2,1)S(1)}, bf16[8,16,2048]{2,1,0:T(8,128)(2,1)}, u32[]{:S(2)}) copy-start(bf16[8,16,2048]{2,1,0:T(8,128)(2,1)} %param.37) | copy-start | bytes 1572868
  7.2 11.1 copy-start.51
  7.2 11.1 copy-start.57
  7.2 24.4 %all-gather.7.cloned.1.call-start = ((), (), s32[]{:S(2)}) async-start(), calls=%async_computation.2 | async-start | bytes 9437184 | tf_op jit(solution)/shard_map/all_gather | solution.py:189
  12.0 165.1 %all-gather.9.cloned.1.call-start = ((), (), s32[]{:S(2)}) async-start(), calls=%async_computation.3 | async-start | bytes 5242880 | tf_op jit(solution)/shard_map/all_gather | solution.py:209
  12.5 29.2 %copy-start.21 = (bf16[16,8,3,512]{3,1,2,0:T(8,128)(2,1)}, bf16[16,8,3,512]{3,1,2,0:T(8,128)(2,1)S(1)}, u32[]{:S(2)}) copy-start(bf16[16,8,3,512]{3,1,2,0:T(8,128)(2,1)S(1)} %copy.94) | copy-start | bytes 1179652
  12.6 9.5 copy-start.30
  23.4 18.3 copy-start.25
  46.3 44.4 %copy-start.56 = (s32[4,2]{0,1:T(2,128)S(1)}, s32[4,2]{0,1:T(2,128)}, u32[]{:S(2)}) copy-start(s32[4,2]{0,1:T(2,128)} %param.22) | copy-start | bytes 100
  46.3 157.0 %all-gather.11.cloned.1.call-start = ((), (), s32[]{:S(2)}) async-start(), calls=%async_computation.4 | async-start | bytes 3145728 | tf_op jit(solution)/shard_map/all_gather | solution.py:195
  47.0 168.1 %all-gather.15.cloned.1.call-start = ((), (), s32[]{:S(2)}) async-start(), calls=%async_computation.6 | async-start | bytes 12582912 | tf_op jit(solution)/shard_map/all_gather | solution.py:196
  47.6 471.1 %all-reduce.15.cloned.1.call-start = ((), (), s32[]{:S(2)}) async-start(), calls=%async_computation.13 | async-start | bytes 17825792 | tf_op jit(solution)/shard_map/psum | solution.py:132
  48.1 36.7 %collective-permute-start = (bf16[1,4,256,512]{3,2,1,0:T(8,128)(2,1)S(1)}, bf16[1,4,256,512]{3,2,1,0:T(8,128)(2,1)}, u32[]{:S(2)}, u32[]{:S(2)}) collective-permute-start(bf16[1,4,256,512]{3,2,1,0:T(8,128)(2,1)S(1)} %bitcast.231), channel_id=1, source_target_pairs={{0,4},{4,0},{8,12},{12,8},{1,5},{5,1},{9,13},{13,9},{2,6},{6,2},{1... | collective-permute-start | bytes 3145736 | tf_op jit(solution)/shard_map/ppermute | solution.py:22
  88.9 66.8 %collective-permute-start.1 = (bf16[2,4,256,512]{3,2,1,0:T(8,128)(2,1)}, bf16[2,4,256,512]{3,2,1,0:T(8,128)(2,1)}, u32[]{:S(2)}, u32[]{:S(2)}) collective-permute-start(bf16[2,4,256,512]{3,2,1,0:T(8,128)(2,1)} %get-tuple-element.52), channel_id=1, source_target_pairs={{0,8},{4,12},{8,0},{12,4},{1,9},{5,13},{9,1},{13,5},{2,10},{6,14},... | collective-permute-start | bytes 6291464 | tf_op jit(solution)/shard_map/ppermute | solution.py:22
  98.4 78.8 %copy-start.17 = (bf16[4,256,4,128]{1,3,2,0:T(8,128)(2,1)}, bf16[4,256,4,128]{1,3,2,0:T(8,128)(2,1)S(1)}, u32[]{:S(2)}) copy-start(bf16[4,256,4,128]{1,3,2,0:T(8,128)(2,1)S(1)} %copy.83) | copy-start | bytes 3145732
  177.1 12.7 copy-start.12
  189.9 12.2 copy-start.40
  202.1 8.5 copy-start.19
  210.6 328.4 %all-gather.13.cloned.1.call-start = ((), (), s32[]{:S(2)}) async-start(), calls=%async_computation.5 | async-start | bytes 12582912 | tf_op jit(solution)/shard_map/all_gather | solution.py:190
  211.2 676.9 %all-reduce.13.cloned.1.call-start = ((), (), s32[]{:S(2)}) async-start(), calls=%async_computation.12 | async-start | bytes 17825792 | tf_op jit(solution)/shard_map/psum | solution.py:132
  215.1 303.7 %copy-start.43 = (f32[4,128]{1,0:T(4,128)S(1)}, f32[4,128]{1,0:T(4,128)}, u32[]{:S(2)}) copy-start(f32[4,128]{1,0:T(4,128)} %copy-done.42) | copy-start | bytes 6148
  215.1 304.7 %copy-start.28 = (bf16[8,16,2048]{2,1,0:T(8,128)(2,1)S(1)}, bf16[8,16,2048]{2,1,0:T(8,128)(2,1)}, u32[]{:S(2)}) copy-start(bf16[8,16,2048]{2,1,0:T(8,128)(2,1)} %param.35) | copy-start | bytes 1572868
  526.2 363.0 %copy-start.46 = (f32[1024]{0:T(1024)}, f32[1024]{0:T(1024)S(1)}, u32[]{:S(2)}) copy-start(f32[1024]{0:T(1024)S(1)} %broadcast_multiply_fusion.1) | copy-start | bytes 12292
  534.0 17.5 copy-start.36
  551.5 16.5 slice-start.6
  556.4 11.6 slice-start.7
  579.0 362.9 %all-gather.17.cloned.1.call-start = ((), (), s32[]{:S(2)}) async-start(), calls=%async_computation.7 | async-start | bytes 5242880 | tf_op jit(solution)/shard_map/all_gather | solution.py:289
  580.4 451.0 %reduce-scatter.5.cloned.1.call-start = ((), (), s32[]{:S(2)}) async-start(), calls=%async_computation.9 | async-start | bytes 10485760 | tf_op jit(solution)/shard_map/reduce_scatter | solution.py:310
  889.2 7.5 copy-start.50
  930.2 190.4 %reduce-scatter.3.cloned.1.call-start = ((), (), s32[]{:S(2)}) async-start(), calls=%async_computation.8 | async-start | bytes 10485760 | tf_op jit(solution)/shard_map/reduce_scatter | solution.py:309
  941.9 12.2 copy-start.18
  959.0 779.1 %all-reduce.11.cloned.1.call-start = ((), (), s32[]{:S(2)}) async-start(), calls=%async_computation.11 | async-start | bytes 35651584 | tf_op jit(solution)/shard_map/psum | solution.py:132
  960.0 19.4 %slice-start.4 = ((s8[8388608]{0:T(1024)(128)(4,1)}), s8[4194304]{0:T(1024)(128)(4,1)S(1)}, s32[]{:S(2)}) async-start(s8[8388608]{0:T(1024)(128)(4,1)} %bitcast.220), calls=%async_computation.18 | async-start | bytes 8388608
  964.7 14.8 slice-start.5
  964.7 14.8 copy-start.15
  1127.4 12.4 copy-start.13
  1127.4 12.4 copy-start.22
  1141.6 721.6 %all-reduce.9.cloned.1.call-start = ((), (), s32[]{:S(2)}) async-start(), calls=%async_computation.10 | async-start | bytes 15204352 | tf_op jit(solution)/shard_map/psum | solution.py:340
  1143.4 9.5 copy-start.24
  1152.9 585.2 %copy-start.45 = (f32[4,128]{1,0:T(4,128)S(1)}, f32[4,128]{1,0:T(4,128)}, u32[]{:S(2)}) copy-start(f32[4,128]{1,0:T(4,128)} %copy-done.42) | copy-start | bytes 6148
  1745.5 15.1 slice-start
  1745.5 9.3 copy-start.4
  1745.5 15.1 slice-start.1
  1754.8 13.0 slice-start.2
  1767.8 109.3 %copy-start.1 = (bf16[8,16,2048]{2,1,0:T(8,128)(2,1)S(1)}, bf16[8,16,2048]{2,1,0:T(8,128)(2,1)}, u32[]{:S(2)}) copy-start(bf16[8,16,2048]{2,1,0:T(8,128)(2,1)} %param.37) | copy-start | bytes 1572868
  1863.1 11.1 copy-start.35
  1863.1 12.0 copy-start.34
  1863.1 13.0 copy-start.33
  (34 other events, 129.3 us)
Sparse Core Ops, SparseCore 0:
  12.1 19.4 all-gather.6
  46.4 83.6 all-gather.8
  131.7 10.2 all-gather.10
  143.4 21.0 all-gather.14
  210.7 307.9 all-reduce.14
  520.1 18.8 all-gather.12
  579.1 308.9 all-reduce.12
  890.5 51.4 all-gather.16
  945.0 86.3 reduce-scatter.4
  1034.3 86.3 reduce-scatter.2
  1141.7 596.3 all-reduce.10
  1745.6 117.5 all-reduce.8
